TPU v7x, 32 devices: a whole 2x2x4 slice. The times are simulated.
32 devices in a mesh: gx: 8 (over z, y), gy: 4 (over x, core).
Axes of the slice: x: 2, y: 2, z: 4, core: 2. Of those that a mesh axis runs over, the one named last changes fastest.
Arguments:
- ice_rhs: float32 [2, 512, 1024], P(None, 'gx', 'gy'), may hold values from -18.6 to 18.6
- ice_guess: float32 [2, 512, 1024], P(None, 'gx', 'gy'), may hold values from -9.3 to 9.3
- ocean_rhs: float32 [512, 1024], P('gx', 'gy'), may hold values from -18.6 to 18.6
- ocean_guess: float32 [512, 1024], P('gx', 'gy'), may hold values from -9.3 to 9.3
- ice_diag: float32 [512, 1024], P('gx', 'gy'), may hold values from 1 to 4
- ice_visc: float32 [512, 1024], P('gx', 'gy'), may hold values from 0.5 to 1.5
- coriolis: float32 [512, 1024], P('gx', 'gy'), may hold values from -1.5 to 1.5
- depth_factor: float32 [512, 1024], P('gx', 'gy'), may hold values from 1 to 3
- wet_mask: int32 [512, 1024], P('gx', 'gy'), may hold values 0 or 1
- ice_mask: int32 [512, 1024], P('gx', 'gy'), may hold values from 0 to 1, as said below
Outputs:
- ice_velocity: float32 [2, 512, 1024], P(None, 'gx', 'gy')
- ocean_level: float32 [512, 1024], P('gx', 'gy')
Inputs may be any that keep to these rules, and one draw needn't show every extreme that they name: `ice_mask`: 1 where sea ice covers the cell.
All inputs are finite; a program needn't handle non-finite values. No bound on the sum of `wet_mask` on one device may be relied on, other than what follows from the above.
Results may differ from a plain program's by a relative error of at most 0.00005.
Values sent between devices are 32-bit elements; how exact they have to be, the bound alone decides.
A program may use at most 64 MiB of HBM per device.

v0:
```python
import jax
import jax.numpy as jnp
from jax import lax
from jax.sharding import PartitionSpec as P


def shifted(value, axis, by):
    size = lax.axis_size(axis)
    pairs = [(i, i + by) for i in range(size) if 0 <= i + by < size]
    return lax.ppermute(value, axis, pairs)


def extended(cells, sides, width, closed):
    for axis, dim in sides:
        count = lax.axis_size(axis)
        ends = count if closed else count - 1
        head = lax.slice_in_dim(cells, 0, width, axis=dim)
        tail = lax.slice_in_dim(cells, cells.shape[dim] - width, cells.shape[dim], axis=dim)
        cells = jnp.concatenate(
            [
                lax.ppermute(tail, axis, [(i, (i + 1) % count) for i in range(ends)]),
                cells,
                lax.ppermute(head, axis, [((i + 1) % count, i) for i in range(ends)]),
            ],
            axis=dim,
        )
    return cells


def inner(left, right):
    return jnp.sum(left * right)


def body(
    ice_rhs,
    ice_guess,
    ocean_rhs,
    ocean_guess,
    ice_diag,
    ice_visc,
    coriolis,
    depth_factor,
    wet_mask,
    ice_mask,
):
    wet = wet_mask.astype(jnp.float32)
    active = wet * ice_mask.astype(jnp.float32)
    act = jnp.stack([active, active, wet])
    root = jnp.stack([ice_visc, ice_visc, depth_factor])
    diag = jnp.stack([ice_diag, ice_diag, jnp.ones_like(ice_diag)])
    inverse = 1.0 / (act * (diag + 4.0 * root * root) + 1.0 - act)
    signs = jnp.array([-1.0, -1.0, 1.0], jnp.float32)[:, None]
    at_top = lax.axis_index("gy") == lax.axis_size("gy") - 1

    def mirror_sections():
        sections = []
        group = lax.axis_size("gx")
        while group % 2 == 0:
            sections.append((group // 2, group, 0))
            group = group // 2
        for offset in range(2, group, 2):
            sections.append((offset, group, 1))
        return sections

    def partner_row(q):
        moving = q[:, :, -1]
        position = lax.axis_index("gx")
        for distance, extent, sort_kind in mirror_sections():
            within = position % extent
            from_above = shifted(moving, "gx", -distance)
            from_below = shifted(moving, "gx", distance)
            if sort_kind == 0:
                take_above = within < distance
                take_below = within >= distance
            else:
                take_above = extent - 1 - 2 * within == distance
                take_below = extent - 1 - 2 * within == -distance
            moving = jnp.where(take_above, from_above, jnp.where(take_below, from_below, moving))
        return moving[:, ::-1]

    def operate(field):
        q = act * root * field
        zonal = extended(q, (("gx", 1),), 1, True)
        merid = extended(q, (("gy", 2),), 1, False)
        ghost = jnp.where(at_top, signs * partner_row(q), 0.0)
        north = jnp.concatenate([merid[:, :, 2:-1], merid[:, :, -1:] + ghost[:, :, None]], axis=2)
        beside_all = zonal[:, 2:, :] + zonal[:, :-2, :] + north + merid[:, :, :-2]
        lap = 4.0 * q - beside_all
        turn = jnp.stack([-coriolis * field[1], coriolis * field[0], jnp.zeros_like(coriolis)])
        return act * (diag * field + root * lap + turn) + (1.0 - act) * field

    start_image = operate(jnp.concatenate([ice_guess, ocean_guess[None]]))
    resid = jnp.concatenate([ice_rhs, ocean_rhs[None]]) - start_image
    r = resid[:2]
    ro = resid[2]
    pre = inverse * resid
    image = operate(pre)
    w_scaled = image[:2]
    az0 = image[2]
    z_scaled = pre[:2]
    z0 = pre[2]

    def merged(values):
        return lax.psum(jnp.stack(values), ("gx", "gy"))

    sums = merged(
        [inner(r, r), inner(w_scaled, r), inner(w_scaled, w_scaled), inner(ro, z0), inner(z0, az0)]
    )
    rr = sums[0]
    beta = jnp.sqrt(rr)
    h11 = sums[1] / rr
    g11 = sums[2] / rr
    h21 = jnp.sqrt(g11 - h11 * h11)
    gamma0 = sums[3]
    alpha0 = gamma0 / sums[4]
    v2 = (w_scaled - h11 * r) / (beta * h21)
    level = ocean_guess + alpha0 * z0
    ro = ro - alpha0 * az0
    znext = inverse[2] * ro
    image2 = operate(jnp.concatenate([inverse[:2] * v2, znext[None]]))
    w2 = image2[:2]
    sums = merged(
        [inner(w2, r), inner(w2, v2), inner(w2, w2), inner(ro, znext), inner(znext, image2[2])]
    )
    h12 = sums[0] / beta
    h22 = sums[1]
    g22 = sums[2]
    gamma1 = sums[3]
    lead = gamma1 / gamma0
    alpha1 = gamma1 / (sums[4] - lead * gamma1 / alpha0)
    p1 = znext + lead * z0
    level = level + alpha1 * p1
    g12 = h11 * h12 + h21 * h22
    first_rhs = beta * h11
    second_rhs = beta * h12
    det = g11 * g22 - g12 * g12
    y_first = (g22 * first_rhs - g12 * second_rhs) / det
    y_second = (g11 * second_rhs - g12 * first_rhs) / det
    velocity = ice_guess + y_first * (z_scaled / beta) + y_second * (inverse[:2] * v2)
    return (velocity, level)


def solution(mesh):
    placed = (
        P(None, "gx", "gy"),
        P(None, "gx", "gy"),
        P("gx", "gy"),
        P("gx", "gy"),
        P("gx", "gy"),
        P("gx", "gy"),
        P("gx", "gy"),
        P("gx", "gy"),
        P("gx", "gy"),
        P("gx", "gy"),
    )
    return jax.shard_map(
        body,
        mesh=mesh,
        in_specs=placed,
        out_specs=(P(None, "gx", "gy"), P("gx", "gy")),
        check_vma=False,
    )
```

profile of v0, /device:TPU:0, one launch (start us, length us, event | category | flops | bytes accessed | tf_op | source)
XLA Modules:
  0.0 202.8 jit_solution(5238889771545232781)
XLA Ops:
  4.0 6.0 %collective-permute-start.4 = (f32[3,64]{1,0:T(4,128)S(1)}, f32[3,64]{1,0:T(4,128)S(1)}, u32[]{:S(2)}, u32[]{:S(2)}) collective-permute-start(f32[3,64]{1,0:T(4,128)S(1)} %get-tuple-element.39), channel_id=1, source_target_pairs={{0,16},{4,20},{8,24},{12,28},{1,17},{5,21},{9,25},{13,29},{2,18},{... | collective-permute-start | bytes 2312 | tf_op jit(solution)/shard_map/ppermute | solution.py:10
  11.3 3.0 %collective-permute-start.9 = (f32[3,64,1]{2,1,0:T(8,128)S(1)}, f32[3,64,1]{2,1,0:T(8,128)S(1)}, u32[]{:S(2)}, u32[]{:S(2)}) collective-permute-start(f32[3,64,1]{2,1,0:T(8,128)S(1)} %get-tuple-element.40), channel_id=1, source_target_pairs={{0,1},{1,2},{2,3},{4,5},{5,6},{6,7},{8,9},{9,10},{10,11},{12,13},{... | collective-permute-start | bytes 2312 | tf_op jit(solution)/shard_map/ppermute | solution.py:21
  14.4 2.4 %collective-permute-start = (f32[3,1,256]{2,1,0:T(1,128)S(1)}, f32[3,1,256]{2,1,0:T(1,128)S(1)}, u32[]{:S(2)}, u32[]{:S(2)}) collective-permute-start(f32[3,1,256]{2,1,0:T(1,128)S(1)} %get-tuple-element.37), channel_id=1, source_target_pairs={{4,0},{8,4},{12,8},{16,12},{20,16},{24,20},{28,24},{0,28},{5,1},{9... | collective-permute-start | bytes 9224 | tf_op jit(solution)/shard_map/ppermute | solution.py:23
  18.1 4.5 %collective-permute-start.6 = (f32[3,64]{1,0:T(4,128)S(1)}, f32[3,64]{1,0:T(4,128)S(1)}, u32[]{:S(2)}, u32[]{:S(2)}) collective-permute-start(f32[3,64]{1,0:T(4,128)S(1)} %select_select_fusion.8), channel_id=1, source_target_pairs={{0,8},{4,12},{8,16},{12,20},{16,24},{20,28},{1,9},{5,13},{9,17},{1... | collective-permute-start | bytes 2312 | tf_op jit(solution)/shard_map/ppermute | solution.py:10
  25.2 4.5 %collective-permute-start.8 = (f32[3,64]{1,0:T(4,128)S(1)}, f32[3,64]{1,0:T(4,128)S(1)}, u32[]{:S(2)}, u32[]{:S(2)}) collective-permute-start(f32[3,64]{1,0:T(4,128)S(1)} %select_select_fusion.7), channel_id=1, source_target_pairs={{0,4},{4,8},{8,12},{12,16},{16,20},{20,24},{24,28},{1,5},{5,9},{9,... | collective-permute-start | bytes 2312 | tf_op jit(solution)/shard_map/ppermute | solution.py:10
  30.1 1.7 collective-permute-start.1
  32.7 3.6 %collective-permute-done.1 = f32[3,1,256]{2,1,0:T(1,128)S(1)} collective-permute-done((f32[3,1,256]{2,1,0:T(1,128)S(1)}, f32[3,1,256]{2,1,0:T(1,128)S(1)}, u32[]{:S(2)}, u32[]{:S(2)}) %collective-permute-start.1) | collective-permute-done | bytes 3104 | tf_op jit(solution)/shard_map/ppermute | solution.py:21
  36.8 1.3 collective-permute-start.13
  38.1 5.4 %collective-permute-start.14 = (f32[3,64]{1,0:T(4,128)S(1)}, f32[3,64]{1,0:T(4,128)S(1)}, u32[]{:S(2)}, u32[]{:S(2)}) collective-permute-start(f32[3,64]{1,0:T(4,128)S(1)} %get-tuple-element.32), channel_id=1, source_target_pairs={{0,16},{4,20},{8,24},{12,28},{1,17},{5,21},{9,25},{13,29},{2,18},{... | collective-permute-start | bytes 2312 | tf_op jit(solution)/shard_map/ppermute | solution.py:10
  43.6 1.3 collective-permute-start.19
  46.2 4.5 %collective-permute-start.16 = (f32[3,64]{1,0:T(4,128)S(1)}, f32[3,64]{1,0:T(4,128)S(1)}, u32[]{:S(2)}, u32[]{:S(2)}) collective-permute-start(f32[3,64]{1,0:T(4,128)S(1)} %select_select_fusion.5), channel_id=1, source_target_pairs={{0,8},{4,12},{8,16},{12,20},{16,24},{20,28},{1,9},{5,13},{9,17},{1... | collective-permute-start | bytes 2312 | tf_op jit(solution)/shard_map/ppermute | solution.py:10
  53.5 4.5 %collective-permute-start.18 = (f32[3,64]{1,0:T(4,128)S(1)}, f32[3,64]{1,0:T(4,128)S(1)}, u32[]{:S(2)}, u32[]{:S(2)}) collective-permute-start(f32[3,64]{1,0:T(4,128)S(1)} %select_select_fusion.4), channel_id=1, source_target_pairs={{0,4},{4,8},{8,12},{12,16},{16,20},{20,24},{24,28},{1,5},{5,9},{9,... | collective-permute-start | bytes 2312 | tf_op jit(solution)/shard_map/ppermute | solution.py:10
  58.1 3.5 %collective-permute-start.10 = (f32[3,1,256]{2,1,0:T(1,128)S(1)}, f32[3,1,256]{2,1,0:T(1,128)S(1)}, u32[]{:S(2)}, u32[]{:S(2)}) collective-permute-start(f32[3,1,256]{2,1,0:T(1,128)S(1)} %get-tuple-element.35), channel_id=1, source_target_pairs={{4,0},{8,4},{12,8},{16,12},{20,16},{24,20},{28,24},{0,28},{5,1},{9... | collective-permute-start | bytes 9224 | tf_op jit(solution)/shard_map/ppermute | solution.py:23
  62.9 5.0 %collective-permute-done.11 = f32[3,1,256]{2,1,0:T(1,128)S(1)} collective-permute-done((f32[3,1,256]{2,1,0:T(1,128)S(1)}, f32[3,1,256]{2,1,0:T(1,128)S(1)}, u32[]{:S(2)}, u32[]{:S(2)}) %collective-permute-start.11) | collective-permute-done | bytes 3104 | tf_op jit(solution)/shard_map/ppermute | solution.py:21
  69.5 3.3 %stack.109 = f32[5]{0:T(128)S(1)} concatenate(f32[1]{0:T(128)} %bitcast.17, f32[1]{0:T(128)} %bitcast.18, f32[1]{0:T(128)} %bitcast.19, f32[1]{0:T(128)} %bitcast.22, f32[1]{0:T(128)} %bitcast.24), dimensions={0} | concatenate | bytes 40 | tf_op jit(solution)/shard_map/stack | solution.py:104
  72.7 36.8 %psum.14 = f32[5]{0:T(128)S(1)} all-reduce(f32[5]{0:T(128)S(1)} %stack.109), channel_id=1, replica_groups=mesh['gx'=8,'gy'=4] {'gx','gy'}, use_global_device_ids=true, to_apply=%region_5.6 | all-reduce | flops 5 | bytes 40 | tf_op jit(solution)/shard_map/psum | solution.py:104
  116.3 5.4 %collective-permute-start.24 = (f32[3,64]{1,0:T(4,128)S(1)}, f32[3,64]{1,0:T(4,128)S(1)}, u32[]{:S(2)}, u32[]{:S(2)}) collective-permute-start(f32[3,64]{1,0:T(4,128)S(1)} %get-tuple-element.27), channel_id=1, source_target_pairs={{0,16},{4,20},{8,24},{12,28},{1,17},{5,21},{9,25},{13,29},{2,18},{... | collective-permute-start | bytes 2312 | tf_op jit(solution)/shard_map/ppermute | solution.py:10
  124.3 5.4 %collective-permute-start.26 = (f32[3,64]{1,0:T(4,128)S(1)}, f32[3,64]{1,0:T(4,128)S(1)}, u32[]{:S(2)}, u32[]{:S(2)}) collective-permute-start(f32[3,64]{1,0:T(4,128)S(1)} %select_select_fusion.2), channel_id=1, source_target_pairs={{0,8},{4,12},{8,16},{12,20},{16,24},{20,28},{1,9},{5,13},{9,17},{1... | collective-permute-start | bytes 2312 | tf_op jit(solution)/shard_map/ppermute | solution.py:10
  132.3 4.8 %collective-permute-start.28 = (f32[3,64]{1,0:T(4,128)S(1)}, f32[3,64]{1,0:T(4,128)S(1)}, u32[]{:S(2)}, u32[]{:S(2)}) collective-permute-start(f32[3,64]{1,0:T(4,128)S(1)} %select_select_fusion.1), channel_id=1, source_target_pairs={{0,4},{4,8},{8,12},{12,16},{16,20},{20,24},{24,28},{1,5},{5,9},{9,... | collective-permute-start | bytes 2312 | tf_op jit(solution)/shard_map/ppermute | solution.py:10
  138.6 3.0 %collective-permute-start.29 = (f32[3,64,1]{2,1,0:T(8,128)S(1)}, f32[3,64,1]{2,1,0:T(8,128)S(1)}, u32[]{:S(2)}, u32[]{:S(2)}) collective-permute-start(f32[3,64,1]{2,1,0:T(8,128)S(1)} %get-tuple-element.28), channel_id=1, source_target_pairs={{0,1},{1,2},{2,3},{4,5},{5,6},{6,7},{8,9},{9,10},{10,11},{12,13},{... | collective-permute-start | bytes 2312 | tf_op jit(solution)/shard_map/ppermute | solution.py:21
  141.6 2.9 %collective-permute-start.20 = (f32[3,1,256]{2,1,0:T(1,128)S(1)}, f32[3,1,256]{2,1,0:T(1,128)S(1)}, u32[]{:S(2)}, u32[]{:S(2)}) collective-permute-start(f32[3,1,256]{2,1,0:T(1,128)S(1)} %get-tuple-element.30), channel_id=1, source_target_pairs={{4,0},{8,4},{12,8},{16,12},{20,16},{24,20},{28,24},{0,28},{5,1},{9... | collective-permute-start | bytes 9224 | tf_op jit(solution)/shard_map/ppermute | solution.py:23
  146.2 4.6 %collective-permute-done.21 = f32[3,1,256]{2,1,0:T(1,128)S(1)} collective-permute-done((f32[3,1,256]{2,1,0:T(1,128)S(1)}, f32[3,1,256]{2,1,0:T(1,128)S(1)}, u32[]{:S(2)}, u32[]{:S(2)}) %collective-permute-start.21) | collective-permute-done | bytes 3104 | tf_op jit(solution)/shard_map/ppermute | solution.py:21
  152.3 3.1 %stack.118 = f32[5]{0:T(128)S(1)} concatenate(f32[1]{0:T(128)} %bitcast.35, f32[1]{0:T(128)} %bitcast.36, f32[1]{0:T(128)} %bitcast.37, f32[1]{0:T(128)} %bitcast.39, f32[1]{0:T(128)} %bitcast.41), dimensions={0} | concatenate | bytes 40 | tf_op jit(solution)/shard_map/stack | solution.py:104
  155.4 38.4 %psum.15 = f32[5]{0:T(128)S(1)} all-reduce(f32[5]{0:T(128)S(1)} %stack.118), channel_id=1, replica_groups=mesh['gx'=8,'gy'=4] {'gx','gy'}, use_global_device_ids=true, to_apply=%region_11.12 | all-reduce | flops 5 | bytes 40 | tf_op jit(solution)/shard_map/psum | solution.py:104
  (110 shorter events, 30.8 us)
Async XLA Ops:
  2.7 14.0 %collective-permute-start.3 = (f32[3,64]{1,0:T(4,128)S(1)}, f32[3,64]{1,0:T(4,128)S(1)}, u32[]{:S(2)}, u32[]{:S(2)}) collective-permute-start(f32[3,64]{1,0:T(4,128)S(1)} %get-tuple-element.39), channel_id=1, source_target_pairs={{16,0},{20,4},{24,8},{28,12},{17,1},{21,5},{25,9},{29,13},{18,2},{... | collective-permute-start | bytes 2312 | tf_op jit(solution)/shard_map/ppermute | solution.py:10
  4.0 12.7 %collective-permute-start.4 = (f32[3,64]{1,0:T(4,128)S(1)}, f32[3,64]{1,0:T(4,128)S(1)}, u32[]{:S(2)}, u32[]{:S(2)}) collective-permute-start(f32[3,64]{1,0:T(4,128)S(1)} %get-tuple-element.39), channel_id=1, source_target_pairs={{0,16},{4,20},{8,24},{12,28},{1,17},{5,21},{9,25},{13,29},{2,18},{... | collective-permute-start | bytes 2312 | tf_op jit(solution)/shard_map/ppermute | solution.py:10
  10.0 22.7 %collective-permute-start.2 = (f32[3,64,1]{2,1,0:T(8,128)S(1)}, f32[3,64,1]{2,1,0:T(8,128)S(1)}, u32[]{:S(2)}, u32[]{:S(2)}) collective-permute-start(f32[3,64,1]{2,1,0:T(8,128)S(1)} %get-tuple-element.41), channel_id=1, source_target_pairs={{1,0},{2,1},{3,2},{5,4},{6,5},{7,6},{9,8},{10,9},{11,10},{13,12},{... | collective-permute-start | bytes 2312 | tf_op jit(solution)/shard_map/ppermute | solution.py:23
  11.3 21.4 %collective-permute-start.9 = (f32[3,64,1]{2,1,0:T(8,128)S(1)}, f32[3,64,1]{2,1,0:T(8,128)S(1)}, u32[]{:S(2)}, u32[]{:S(2)}) collective-permute-start(f32[3,64,1]{2,1,0:T(8,128)S(1)} %get-tuple-element.40), channel_id=1, source_target_pairs={{0,1},{1,2},{2,3},{4,5},{5,6},{6,7},{8,9},{9,10},{10,11},{12,13},{... | collective-permute-start | bytes 2312 | tf_op jit(solution)/shard_map/ppermute | solution.py:21
  14.4 18.4 %collective-permute-start = (f32[3,1,256]{2,1,0:T(1,128)S(1)}, f32[3,1,256]{2,1,0:T(1,128)S(1)}, u32[]{:S(2)}, u32[]{:S(2)}) collective-permute-start(f32[3,1,256]{2,1,0:T(1,128)S(1)} %get-tuple-element.37), channel_id=1, source_target_pairs={{4,0},{8,4},{12,8},{16,12},{20,16},{24,20},{28,24},{0,28},{5,1},{9... | collective-permute-start | bytes 9224 | tf_op jit(solution)/shard_map/ppermute | solution.py:23
  25.2 6.6 %collective-permute-start.8 = (f32[3,64]{1,0:T(4,128)S(1)}, f32[3,64]{1,0:T(4,128)S(1)}, u32[]{:S(2)}, u32[]{:S(2)}) collective-permute-start(f32[3,64]{1,0:T(4,128)S(1)} %select_select_fusion.7), channel_id=1, source_target_pairs={{0,4},{4,8},{8,12},{12,16},{16,20},{20,24},{24,28},{1,5},{5,9},{9,... | collective-permute-start | bytes 2312 | tf_op jit(solution)/shard_map/ppermute | solution.py:10
  30.1 6.3 %collective-permute-start.1 = (f32[3,1,256]{2,1,0:T(1,128)S(1)}, f32[3,1,256]{2,1,0:T(1,128)S(1)}, u32[]{:S(2)}, u32[]{:S(2)}) collective-permute-start(f32[3,1,256]{2,1,0:T(1,128)S(1)} %get-tuple-element.38), channel_id=1, source_target_pairs={{0,4},{4,8},{8,12},{12,16},{16,20},{20,24},{24,28},{28,0},{1,5},{5... | collective-permute-start | bytes 9224 | tf_op jit(solution)/shard_map/ppermute | solution.py:21
  36.8 8.1 %collective-permute-start.13 = (f32[3,64]{1,0:T(4,128)S(1)}, f32[3,64]{1,0:T(4,128)S(1)}, u32[]{:S(2)}, u32[]{:S(2)}) collective-permute-start(f32[3,64]{1,0:T(4,128)S(1)} %get-tuple-element.32), channel_id=1, source_target_pairs={{16,0},{20,4},{24,8},{28,12},{17,1},{21,5},{25,9},{29,13},{18,2},{... | collective-permute-start | bytes 2312 | tf_op jit(solution)/shard_map/ppermute | solution.py:10
  38.1 6.8 %collective-permute-start.14 = (f32[3,64]{1,0:T(4,128)S(1)}, f32[3,64]{1,0:T(4,128)S(1)}, u32[]{:S(2)}, u32[]{:S(2)}) collective-permute-start(f32[3,64]{1,0:T(4,128)S(1)} %get-tuple-element.32), channel_id=1, source_target_pairs={{0,16},{4,20},{8,24},{12,28},{1,17},{5,21},{9,25},{13,29},{2,18},{... | collective-permute-start | bytes 2312 | tf_op jit(solution)/shard_map/ppermute | solution.py:10
  43.6 18.4 %collective-permute-start.19 = (f32[3,64,1]{2,1,0:T(8,128)S(1)}, f32[3,64,1]{2,1,0:T(8,128)S(1)}, u32[]{:S(2)}, u32[]{:S(2)}) collective-permute-start(f32[3,64,1]{2,1,0:T(8,128)S(1)} %get-tuple-element.33), channel_id=1, source_target_pairs={{0,1},{1,2},{2,3},{4,5},{5,6},{6,7},{8,9},{9,10},{10,11},{12,13},{... | collective-permute-start | bytes 2312 | tf_op jit(solution)/shard_map/ppermute | solution.py:21
  44.9 7.3 %collective-permute-start.15 = (f32[3,64]{1,0:T(4,128)S(1)}, f32[3,64]{1,0:T(4,128)S(1)}, u32[]{:S(2)}, u32[]{:S(2)}) collective-permute-start(f32[3,64]{1,0:T(4,128)S(1)} %select_select_fusion.5), channel_id=1, source_target_pairs={{8,0},{12,4},{16,8},{20,12},{24,16},{28,20},{9,1},{13,5},{17,9},{2... | collective-permute-start | bytes 2312 | tf_op jit(solution)/shard_map/ppermute | solution.py:10
  50.9 11.0 %collective-permute-start.12 = (f32[3,64,1]{2,1,0:T(8,128)S(1)}, f32[3,64,1]{2,1,0:T(8,128)S(1)}, u32[]{:S(2)}, u32[]{:S(2)}) collective-permute-start(f32[3,64,1]{2,1,0:T(8,128)S(1)} %get-tuple-element.34), channel_id=1, source_target_pairs={{1,0},{2,1},{3,2},{5,4},{6,5},{7,6},{9,8},{10,9},{11,10},{13,12},{... | collective-permute-start | bytes 2312 | tf_op jit(solution)/shard_map/ppermute | solution.py:23
  52.2 9.4 %collective-permute-start.17 = (f32[3,64]{1,0:T(4,128)S(1)}, f32[3,64]{1,0:T(4,128)S(1)}, u32[]{:S(2)}, u32[]{:S(2)}) collective-permute-start(f32[3,64]{1,0:T(4,128)S(1)} %select_select_fusion.4), channel_id=1, source_target_pairs={{4,0},{8,4},{12,8},{16,12},{20,16},{24,20},{28,24},{5,1},{9,5},{13... | collective-permute-start | bytes 2312 | tf_op jit(solution)/shard_map/ppermute | solution.py:10
  53.5 8.1 %collective-permute-start.18 = (f32[3,64]{1,0:T(4,128)S(1)}, f32[3,64]{1,0:T(4,128)S(1)}, u32[]{:S(2)}, u32[]{:S(2)}) collective-permute-start(f32[3,64]{1,0:T(4,128)S(1)} %select_select_fusion.4), channel_id=1, source_target_pairs={{0,4},{4,8},{8,12},{12,16},{16,20},{20,24},{24,28},{1,5},{5,9},{9,... | collective-permute-start | bytes 2312 | tf_op jit(solution)/shard_map/ppermute | solution.py:10
  61.6 6.3 %collective-permute-start.11 = (f32[3,1,256]{2,1,0:T(1,128)S(1)}, f32[3,1,256]{2,1,0:T(1,128)S(1)}, u32[]{:S(2)}, u32[]{:S(2)}) collective-permute-start(f32[3,1,256]{2,1,0:T(1,128)S(1)} %get-tuple-element.36), channel_id=1, source_target_pairs={{0,4},{4,8},{8,12},{12,16},{16,20},{20,24},{24,28},{28,0},{1,5},{5... | collective-permute-start | bytes 9224 | tf_op jit(solution)/shard_map/ppermute | solution.py:21
  115.0 6.8 %collective-permute-start.23 = (f32[3,64]{1,0:T(4,128)S(1)}, f32[3,64]{1,0:T(4,128)S(1)}, u32[]{:S(2)}, u32[]{:S(2)}) collective-permute-start(f32[3,64]{1,0:T(4,128)S(1)} %get-tuple-element.27), channel_id=1, source_target_pairs={{16,0},{20,4},{24,8},{28,12},{17,1},{21,5},{25,9},{29,13},{18,2},{... | collective-permute-start | bytes 2312 | tf_op jit(solution)/shard_map/ppermute | solution.py:10
  116.3 6.7 %collective-permute-start.24 = (f32[3,64]{1,0:T(4,128)S(1)}, f32[3,64]{1,0:T(4,128)S(1)}, u32[]{:S(2)}, u32[]{:S(2)}) collective-permute-start(f32[3,64]{1,0:T(4,128)S(1)} %get-tuple-element.27), channel_id=1, source_target_pairs={{0,16},{4,20},{8,24},{12,28},{1,17},{5,21},{9,25},{13,29},{2,18},{... | collective-permute-start | bytes 2312 | tf_op jit(solution)/shard_map/ppermute | solution.py:10
  123.1 6.7 %collective-permute-start.25 = (f32[3,64]{1,0:T(4,128)S(1)}, f32[3,64]{1,0:T(4,128)S(1)}, u32[]{:S(2)}, u32[]{:S(2)}) collective-permute-start(f32[3,64]{1,0:T(4,128)S(1)} %select_select_fusion.2), channel_id=1, source_target_pairs={{8,0},{12,4},{16,8},{20,12},{24,16},{28,20},{9,1},{13,5},{17,9},{2... | collective-permute-start | bytes 2312 | tf_op jit(solution)/shard_map/ppermute | solution.py:10
  124.3 6.7 %collective-permute-start.26 = (f32[3,64]{1,0:T(4,128)S(1)}, f32[3,64]{1,0:T(4,128)S(1)}, u32[]{:S(2)}, u32[]{:S(2)}) collective-permute-start(f32[3,64]{1,0:T(4,128)S(1)} %select_select_fusion.2), channel_id=1, source_target_pairs={{0,8},{4,12},{8,16},{12,20},{16,24},{20,28},{1,9},{5,13},{9,17},{1... | collective-permute-start | bytes 2312 | tf_op jit(solution)/shard_map/ppermute | solution.py:10
  131.0 13.4 %collective-permute-start.27 = (f32[3,64]{1,0:T(4,128)S(1)}, f32[3,64]{1,0:T(4,128)S(1)}, u32[]{:S(2)}, u32[]{:S(2)}) collective-permute-start(f32[3,64]{1,0:T(4,128)S(1)} %select_select_fusion.1), channel_id=1, source_target_pairs={{4,0},{8,4},{12,8},{16,12},{20,16},{24,20},{28,24},{5,1},{9,5},{13... | collective-permute-start | bytes 2312 | tf_op jit(solution)/shard_map/ppermute | solution.py:10
  132.3 12.3 %collective-permute-start.28 = (f32[3,64]{1,0:T(4,128)S(1)}, f32[3,64]{1,0:T(4,128)S(1)}, u32[]{:S(2)}, u32[]{:S(2)}) collective-permute-start(f32[3,64]{1,0:T(4,128)S(1)} %select_select_fusion.1), channel_id=1, source_target_pairs={{0,4},{4,8},{8,12},{12,16},{16,20},{20,24},{24,28},{1,5},{5,9},{9,... | collective-permute-start | bytes 2312 | tf_op jit(solution)/shard_map/ppermute | solution.py:10
  137.3 7.7 %collective-permute-start.22 = (f32[3,64,1]{2,1,0:T(8,128)S(1)}, f32[3,64,1]{2,1,0:T(8,128)S(1)}, u32[]{:S(2)}, u32[]{:S(2)}) collective-permute-start(f32[3,64,1]{2,1,0:T(8,128)S(1)} %get-tuple-element.29), channel_id=1, source_target_pairs={{1,0},{2,1},{3,2},{5,4},{6,5},{7,6},{9,8},{10,9},{11,10},{13,12},{... | collective-permute-start | bytes 2312 | tf_op jit(solution)/shard_map/ppermute | solution.py:23
  138.6 6.4 %collective-permute-start.29 = (f32[3,64,1]{2,1,0:T(8,128)S(1)}, f32[3,64,1]{2,1,0:T(8,128)S(1)}, u32[]{:S(2)}, u32[]{:S(2)}) collective-permute-start(f32[3,64,1]{2,1,0:T(8,128)S(1)} %get-tuple-element.28), channel_id=1, source_target_pairs={{0,1},{1,2},{2,3},{4,5},{5,6},{6,7},{8,9},{9,10},{10,11},{12,13},{... | collective-permute-start | bytes 2312 | tf_op jit(solution)/shard_map/ppermute | solution.py:21
  144.5 6.3 %collective-permute-start.21 = (f32[3,1,256]{2,1,0:T(1,128)S(1)}, f32[3,1,256]{2,1,0:T(1,128)S(1)}, u32[]{:S(2)}, u32[]{:S(2)}) collective-permute-start(f32[3,1,256]{2,1,0:T(1,128)S(1)} %get-tuple-element.31), channel_id=1, source_target_pairs={{0,4},{4,8},{8,12},{12,16},{16,20},{20,24},{24,28},{28,0},{1,5},{5... | collective-permute-start | bytes 9224 | tf_op jit(solution)/shard_map/ppermute | solution.py:21
  (15 other events, 64.8 us)
where the time goes:
time: 204 us; the launch traced here: 203 us
  starting transfers between devices  78.7 us (39%)
  blocking collectives  75.1 us (37%)
  waiting for transfers between devices  19.2 us (9%)
  between operations  12.9 us (6%)
  local copies, waits for them, and re-layouts  9.87 us (5%)
  other arithmetic  6.94 us (3%)
    psum x2, blocking collectives, merged(): return lax.psum(jnp.stack(values), ('gx', 'gy'))  75.1 us
    ppermute x18, starting transfers between devices, shifted(): return lax.ppermute(value, axis, pairs)  56.8 us
    ppermute x6, waiting for transfers between devices, extended(): lax.ppermute(tail, axis, [(i, (i + 1) % count) for i in range(ends)])  13.2 us
    ppermute x6, starting transfers between devices, extended(): lax.ppermute(head, axis, [((i + 1) % count, i) for i in range(ends)])  12.6 us
    ppermute x6, starting transfers between devices, extended(): lax.ppermute(tail, axis, [(i, (i + 1) % count) for i in range(ends)])  9.27 us
    another operation x2, local copies, waits for them, and re-layouts, merged(): return lax.psum(jnp.stack(values), ('gx', 'gy'))  6.33 us
  transfers between devices with their start and end apart: 30, of which 8 were waited for; matrix products, arithmetic and copies ran while one was open for 1% of the time, Pallas kernels for 0%

commit v1 on v0

v1 whole, which is shorter than its diff:
```python
import functools

import jax
import jax.numpy as jnp
from jax import lax
from jax.experimental import pallas as pl
from jax.experimental.pallas import tpu as pltpu
from jax.sharding import PartitionSpec as P

MESH = pl.DeviceIdType.MESH
LANES = 128
ROWS = 32
WIDTHS = (3, 3, 3, 2, 2, 2, 2, 2, 2, 2, 2)
PLACES = tuple(sum(WIDTHS[:i]) for i in range(len(WIDTHS)))
EAST, WEST, NORTH, SOUTH, NE, NW, SE, SW = range(8)
FLAT_LIMIT = 64
SUMS = 9


def flipped_rows(x):
    tiles = [x[k : k + 8] for k in range(0, x.shape[0], 8)][::-1]
    x = jnp.concatenate(tiles, axis=0)
    place = lax.broadcasted_iota(jnp.int32, x.shape, 0)
    size = x.shape[0]
    for bit in (1, 2, 4):
        x = jnp.where((place & bit) == 0, pltpu.roll(x, size - bit, 0), pltpu.roll(x, bit, 0))
    return x


def flipped_lanes(x):
    place = lax.broadcasted_iota(jnp.int32, x.shape, 1)
    for bit in (1, 2, 4, 8, 16, 32, 64):
        x = jnp.where((place & bit) == 0, pltpu.roll(x, LANES - bit, 1), pltpu.roll(x, bit, 1))
    return x


def rolled(x, by, axis):
    return pltpu.roll(x, by % x.shape[axis], axis)


def beside(x):
    return (rolled(x, 1, 0) + rolled(x, -1, 0)) + (rolled(x, 1, 1) + rolled(x, -1, 1))


def two_by_two(g11, g12, g22, f1, f2):
    det = g11 * g22 - g12 * g12
    good = det > 0.0
    safe = jnp.where(good, det, 1.0)
    first = jnp.where(good, (g22 * f1 - g12 * f2) / safe, f1 / g11)
    second = jnp.where(good, (g11 * f2 - g12 * f1) / safe, 0.0)
    return first, second


def kernel(sizes, *refs):
    gx, gy, rows, cols = sizes
    total = gx * gy
    ins = refs[:10]
    out_ice, out_ocean = refs[10:12]
    held = refs[12:22]
    (
        ext, inv_ref, send_e, send_w, send_n, send_s, send_ne, send_nw,
        recv_e, recv_w, recv_n, recv_s, recv_corner, wide_e, wide_w, sums,
        in_sem, send_sem, recv_sem, sum_send, sum_recv,
    ) = refs[22:]
    x = lax.axis_index("gx")
    y = lax.axis_index("gy")
    me = x * gy + y
    top = y == gy - 1
    bottom = y == 0

    loads = [pltpu.make_async_copy(ins[k], held[k], in_sem.at[k]) for k in range(10)]
    for load in loads:
        load.start()

    flat = total <= FLAT_LIMIT
    barrier = pltpu.get_barrier_semaphore()

    def greet(px, py):
        pl.semaphore_signal(barrier, inc=1, device_id=(px, py), device_id_type=MESH)

    east, west = lax.rem(x + 1, gx), lax.rem(x + gx - 1, gx)
    if flat:
        @pl.loop(1, total)
        def _(k):
            other = lax.rem(me + k, total)
            greet(other // gy, lax.rem(other, gy))
    else:
        @pl.loop(1, gx)
        def _(k):
            greet(lax.rem(x + k, gx), y)

        @pl.loop(1, gy)
        def _(k):
            greet(x, lax.rem(y + k, gy))

        @pl.when(jnp.logical_not(top))
        def _():
            greet(east, y + 1)
            greet(west, y + 1)

        @pl.when(jnp.logical_not(bottom))
        def _():
            greet(east, y - 1)
            greet(west, y - 1)

    @pl.when(bottom)
    def _():
        recv_s[...] = jnp.zeros_like(recv_s)
        recv_corner[SE - NE] = jnp.zeros((ROWS, LANES), jnp.float32)
        recv_corner[SW - NE] = jnp.zeros((ROWS, LANES), jnp.float32)

    for load in loads:
        load.wait()
    rhs, guess, orhs, oguess, mass, visc, cor, depth, wetm, icem = held
    wet = wetm[...].astype(jnp.float32)
    active = wet * icem[...].astype(jnp.float32)
    visc = visc[...]
    depth = depth[...]
    mass = mass[...]
    cor = cor[...]
    gu, gv, gs = guess[0], guess[1], oguess[...]
    ai = active * visc
    ao = wet * depth
    full_i = active * (mass + 4.0 * visc * visc) + 1.0 - active
    full_o = wet * (1.0 + 4.0 * depth * depth) + 1.0 - wet
    pi = 1.0 / full_i
    po = 1.0 / full_o
    inv_ref[0] = pi
    inv_ref[1] = po
    ac = active * cor
    fields = [
        ai * gu,
        ai * gv,
        ao * gs,
        rhs[0] - (full_i * gu - ac * gv),
        rhs[1] - (full_i * gv + ac * gu),
        orhs[...] - full_o * gs,
        ai,
        ao,
        ai * pi,
        ao * po,
        ac * pi,
    ]
    for k, field in enumerate(fields):
        ext[k, 0:rows, 0:cols] = field

    send_e[...] = jnp.zeros_like(send_e)
    send_w[...] = jnp.zeros_like(send_w)
    for k, (width, place) in enumerate(zip(WIDTHS, PLACES)):
        send_w[place : place + width, :] = ext[k, 0:width, 0:cols]
        start = ROWS - place - width
        send_e[start : start + width, :] = ext[k, rows - width : rows, 0:cols]
    lane = lax.broadcasted_iota(jnp.int32, (rows, LANES), 1)
    low = jnp.zeros((rows, LANES), jnp.float32)
    high = jnp.zeros((rows, LANES), jnp.float32)
    for k, (width, place) in enumerate(zip(WIDTHS, PLACES)):
        first = ext[k, 0:rows, 0:LANES]
        last = ext[k, 0:rows, cols - LANES : cols]
        low = jnp.where((lane >= place) & (lane < place + width), rolled(first, place, 1), low)
        start = LANES - place - width
        high = jnp.where((lane >= start) & (lane < start + width), rolled(last, -place, 1), high)
    send_s[...] = low

    @pl.when(jnp.logical_not(top))
    def _():
        send_n[...] = high
        send_ne[...] = send_e[:, cols - LANES : cols]
        send_nw[...] = send_w[:, cols - LANES : cols]

    def negated(place):
        return (place < 6) | ((place >= 9) & (place < 13))

    @pl.when(top)
    def _():
        sign = jnp.where(negated(lane), -1.0, 1.0)
        send_n[...] = sign * flipped_lanes(flipped_rows(high))
        row = lax.broadcasted_iota(jnp.int32, (ROWS, LANES), 0)
        e_side = flipped_lanes(flipped_rows(send_e[:, cols - LANES : cols]))
        send_ne[...] = jnp.where(negated(row), -e_side, e_side)
        w_side = flipped_lanes(flipped_rows(send_w[:, cols - LANES : cols]))
        send_nw[...] = jnp.where(negated(ROWS - 1 - row), -w_side, w_side)

    if flat:
        pl.semaphore_wait(barrier, total - 1)
    else:
        diagonals = 2 * (jnp.where(top, 0, 1) + jnp.where(bottom, 0, 1))
        pl.semaphore_wait(barrier, gx - 1 + gy - 1 + diagonals)

    def copy(source, where, slot, px, py):
        return pltpu.make_async_remote_copy(
            src_ref=source,
            dst_ref=where,
            send_sem=send_sem.at[slot],
            recv_sem=recv_sem.at[slot],
            device_id=(px, py),
            device_id_type=MESH,
        )

    mirror = gx - 1 - x
    fold_e = lax.rem(mirror + gx - 1, gx)
    fold_w = lax.rem(mirror + 1, gx)
    corner = [recv_corner.at[k] for k in range(4)]
    to_e = copy(send_e, recv_w, WEST, east, y)
    to_w = copy(send_w, recv_e, EAST, west, y)
    plain_n = [
        copy(send_n, recv_s, SOUTH, x, y + 1),
        copy(send_ne, corner[SW - NE], SW, east, y + 1),
        copy(send_nw, corner[SE - NE], SE, west, y + 1),
    ]
    fold_n = copy(send_n, recv_n, NORTH, mirror, y)
    fold_ne = copy(send_ne, corner[NE - NE], NE, fold_e, y)
    fold_nw = copy(send_nw, corner[NW - NE], NW, fold_w, y)
    plain_s = [
        copy(send_s, recv_n, NORTH, x, y - 1),
        copy(send_e.at[:, 0:LANES], corner[NW - NE], NW, east, y - 1),
        copy(send_w.at[:, 0:LANES], corner[NE - NE], NE, west, y - 1),
    ]
    away_e = top & (fold_e != x)
    away_w = top & (fold_w != x)

    to_e.start()
    to_w.start()

    @pl.when(top)
    def _():
        fold_n.start()

    @pl.when(away_e)
    def _():
        fold_ne.start()

    @pl.when(away_w)
    def _():
        fold_nw.start()

    @pl.when(top & (fold_e == x))
    def _():
        recv_corner[NE - NE] = send_ne[...]

    @pl.when(top & (fold_w == x))
    def _():
        recv_corner[NW - NE] = send_nw[...]

    @pl.when(jnp.logical_not(top))
    def _():
        for c in plain_n:
            c.start()

    @pl.when(jnp.logical_not(bottom))
    def _():
        for c in plain_s:
            c.start()

    @pl.when(jnp.logical_not(bottom))
    def _():
        for c in plain_n:
            c.wait_recv()

    plain_s[0].wait_recv()

    @pl.when(jnp.logical_not(top & (fold_e == x)))
    def _():
        plain_s[2].wait_recv()

    @pl.when(jnp.logical_not(top & (fold_w == x)))
    def _():
        plain_s[1].wait_recv()

    to_e.wait_recv()
    to_w.wait_recv()

    from_n = recv_n[...]
    from_s = recv_s[...]
    wide_e[:, 0:cols] = recv_e[...]
    wide_w[:, 0:cols] = recv_w[...]
    side = lax.broadcasted_iota(jnp.int32, (ROWS, LANES), 1) < LANES // 2
    wide_e[:, cols : cols + LANES] = jnp.where(side, recv_corner[NE - NE], recv_corner[SE - NE])
    wide_w[:, cols : cols + LANES] = jnp.where(side, recv_corner[NW - NE], recv_corner[SW - NE])
    upper = lax.broadcasted_iota(jnp.int32, (8, cols + LANES), 0) < 4
    for k, place in enumerate(PLACES):
        ext[k, 0:rows, cols : cols + LANES] = jnp.where(
            lane < LANES // 2, rolled(from_n, -place, 1), rolled(from_s, place, 1)
        )
        end = ROWS - place
        ext[k, rows : rows + 8, :] = jnp.where(
            upper, wide_e[place : place + 8, :], wide_w[end - 8 : end, :]
        )

    ai, ao, si, so, c = (ext[k] for k in range(6, 11))
    ru = ext[3] + ai * beside(ext[0])
    rv = ext[4] + ai * beside(ext[1])
    rs = ext[5] + ao * beside(ext[2])
    nu = ai * beside(si * ru) + c * rv
    nv = ai * beside(si * rv) - c * ru
    ns = ao * beside(so * rs)
    mu = ai * beside(si * nu) + c * nv
    mv = ai * beside(si * nv) - c * nu
    ms = ao * beside(so * ns)

    def own(value):
        return value[0:rows, 0:cols]

    ru, rv, rs, nu, nv, ns, mu, mv, ms = map(own, (ru, rv, rs, nu, nv, ns, mu, mv, ms))
    pi, po = inv_ref[0], inv_ref[1]
    e1u, e1v, e1s = ru - nu, rv - nv, rs - ns
    e2u, e2v, e2s = nu - mu, nv - mv, ns - ms
    prs, pns = po * rs, po * ns
    products = [
        e1u * e1u + e1v * e1v,
        e1u * e2u + e1v * e2v,
        e2u * e2u + e2v * e2v,
        e1u * ru + e1v * rv,
        e2u * ru + e2v * rv,
        prs * e1s,
        pns * e1s,
        pns * e2s,
        pns * rs,
    ]
    spot = lax.broadcasted_iota(jnp.int32, (1, LANES), 1)
    packed = jnp.zeros((1, LANES), jnp.float32)
    for k, product in enumerate(products):
        packed = jnp.where(spot == k, jnp.sum(product, keepdims=True), packed)

    def exchange(slot, count, mine, device, number):
        slot[mine] = packed_now[0]

        def one(k):
            return pltpu.make_async_remote_copy(
                src_ref=slot.at[mine],
                dst_ref=slot.at[mine],
                send_sem=sum_send.at[number],
                recv_sem=sum_recv.at[number],
                device_id=device(k),
                device_id_type=MESH,
            )

        @pl.loop(1, count)
        def _(k):
            one(k).start()

        most = slot.at[pl.ds(0, count - 1)]
        pltpu.make_async_copy(most, most, sum_recv.at[number]).wait()
        result = jnp.sum(slot[...], axis=0)
        pltpu.make_async_copy(most, most, sum_send.at[number]).wait()
        return result

    packed_now = [packed]
    if flat:
        def anyone(k):
            other = lax.rem(me + k, total)
            return (other // gy, lax.rem(other, gy))

        packed = exchange(sums, total, me, anyone, 0)
    else:
        packed_now[0] = exchange(
            sums.at[pl.ds(0, gx)], gx, x, lambda k: (lax.rem(x + k, gx), y), 0
        )
        packed = exchange(
            sums.at[pl.ds(gx, gy)], gy, y, lambda k: (x, lax.rem(y + k, gy)), 1
        )
    s = [
        jnp.sum(jnp.where(spot == k, packed, 0.0), axis=1, keepdims=True) for k in range(SUMS)
    ]
    y1, y2 = two_by_two(s[0], s[1], s[2], s[3], s[4])
    d1, d2 = two_by_two(s[5], s[6], s[7], s[5] + s[8], s[8])
    out_ice[0] = held[1][0] + pi * (y1 * ru + y2 * nu)
    out_ice[1] = held[1][1] + pi * (y1 * rv + y2 * nv)
    out_ocean[...] = held[3][...] + d1 * prs + d2 * pns

    to_e.wait_send()
    to_w.wait_send()

    @pl.when(top)
    def _():
        fold_n.wait_send()

    @pl.when(away_e)
    def _():
        fold_ne.wait_send()

    @pl.when(away_w)
    def _():
        fold_nw.wait_send()

    @pl.when(jnp.logical_not(top))
    def _():
        for c in plain_n:
            c.wait_send()

    @pl.when(jnp.logical_not(bottom))
    def _():
        for c in plain_s:
            c.wait_send()


def solution(mesh):
    gx, gy = mesh.shape["gx"], mesh.shape["gy"]

    def body(*args):
        _, rows, cols = args[0].shape
        slots = gx * gy if gx * gy <= FLAT_LIMIT else gx + gy
        f32 = jnp.float32
        edge = pltpu.VMEM((rows, LANES), f32)
        strip = pltpu.VMEM((ROWS, cols), f32)
        corner = pltpu.VMEM((ROWS, LANES), f32)
        wide = pltpu.VMEM((ROWS, cols + LANES), f32)
        return pl.pallas_call(
            functools.partial(kernel, (gx, gy, rows, cols)),
            out_shape=(
                jax.ShapeDtypeStruct((2, rows, cols), f32),
                jax.ShapeDtypeStruct((rows, cols), f32),
            ),
            in_specs=[pl.BlockSpec(memory_space=pl.ANY)] * 10,
            out_specs=(pl.BlockSpec(memory_space=pltpu.VMEM),) * 2,
            scratch_shapes=[pltpu.VMEM(a.shape, a.dtype) for a in args]
            + [
                pltpu.VMEM((len(WIDTHS), rows + 8, cols + LANES), f32),
                pltpu.VMEM((2, rows, cols), f32),
                strip, strip, edge, edge, corner, corner,
                strip, strip, edge, edge, pltpu.VMEM((4, ROWS, LANES), f32), wide, wide,
                pltpu.VMEM((slots, 1, LANES), f32),
                pltpu.SemaphoreType.DMA((10,)),
                pltpu.SemaphoreType.DMA((8,)),
                pltpu.SemaphoreType.DMA((8,)),
                pltpu.SemaphoreType.DMA((2,)),
                pltpu.SemaphoreType.DMA((2,)),
            ],
            compiler_params=pltpu.CompilerParams(collective_id=0, has_side_effects=True),
            name="picard",
        )(*args)

    grid3, grid2 = P(None, "gx", "gy"), P("gx", "gy")
    return jax.shard_map(
        body,
        mesh=mesh,
        in_specs=(grid3, grid3) + (grid2,) * 8,
        out_specs=(grid3, grid2),
        check_vma=False,
    )
```

time: 204 us -> 21.1 us (0.10)
  starting transfers between devices: 78.7 us -> 0 us
  blocking collectives: 75.1 us -> 0 us
  waiting for transfers between devices: 19.2 us -> 0 us
  Pallas kernels: 0 us -> 18.1 us
  between operations: 12.9 us -> 0.65 us
  local copies, waits for them, and re-layouts: 9.87 us -> 2.23 us
  other arithmetic: 6.94 us -> 0 us
    ppermute x30 -> x0, starting transfers between devices: 78.7 us -> none  [the longest x18 56.8 us: shifted(): return lax.ppermute(value, axis, pairs)]
    psum x2 -> x0, blocking collectives: 75.1 us -> none  [merged(): return lax.psum(jnp.stack(values), ('gx', 'gy'))]
    ppermute x30 -> x0, waiting for transfers between devices: 19.2 us -> none  [the longest x6 13.2 us: extended(): lax.ppermute(tail, axis, [(i, (i + 1) % count) for i in range(ends)])]
    pallas_call x0 -> x1, Pallas kernels: none -> 18.1 us  [body(): pl.pallas_call(functools.partial(kernel, (gx, gy, rows, cols)), out_shape...]
    another operation x4 -> x0, local copies, waits for them, and re-layouts: 6.48 us -> none  [the longest x2 6.33 us: merged(): return lax.psum(jnp.stack(values), ('gx', 'gy'))]
    reduce_sum x4 -> x0, other arithmetic: 2.71 us -> none  [inner(): return jnp.sum(left * right)]
    slice x11 -> x0, local copies, waits for them, and re-layouts: 2.16 us -> none  [the longest x1 0.66 us: body(): alpha0 = gamma0 / sums[4]]
  transfers between devices with their start and end apart: 30 -> 0, of which waited for: 8 -> 0; matrix products, arithmetic and copies ran while one was open for 1% -> 0% of each run, Pallas kernels for 0% -> 0%
where the time goes in v1:
time: 21.1 us; the launch traced here: 21 us
  Pallas kernels  18.1 us (86%)
  local copies, waits for them, and re-layouts  2.23 us (11%)
  between operations  0.65 us (3%)
    pallas_call x1, Pallas kernels, body(): pl.pallas_call(functools.partial(kernel, (gx, gy, rows, cols)), out_shape...  18.1 us
    unnamed x4, local copies, waits for them, and re-layouts  2.23 us

profile of v1, /device:TPU:0, one launch (start us, length us, event | category | flops | bytes accessed | tf_op | source)
XLA Modules:
  0.0 21.0 jit_solution(1299659371635198481)
XLA Ops:
  0.6 18.1 %picard.1 = (f32[2,64,256]{2,1,0:T(8,128)}, f32[64,256]{1,0:T(8,128)}) custom-call(f32[2,64,256]{2,1,0:T(8,128)} %refs_0_.1, f32[2,64,256]{2,1,0:T(8,128)} %refs_1_.1, f32[64,256]{1,0:T(8,128)} %refs_2_.1, f32[64,256]{1,0:T(8,128)} %refs_3_.1, f32[64,256]{1,0:T(8,128)} %refs_4_.1, f32[64,256]{1,0:T(8,128)} %refs_5_.1, f32[64,256]{1,0:T(8,128)} %refs_6_.1, ...), custom_call_target="tpu_custom_call" | custom-call | tf_op jit(solution)/shard_map/picard/pallas_call | solution.py:407
  18.7 0.0 copy-start
  18.7 1.6 %copy.14 = f32[2,64,256]{2,1,0:T(8,128)} copy(f32[2,64,256]{2,1,0:T(8,128)} %get-tuple-element.4) | data formatting | bytes 262144
  20.3 0.0 copy-done
  20.3 0.6 %copy.15 = f32[64,256]{1,0:T(8,128)} copy(f32[64,256]{1,0:T(8,128)S(1)} %copy-done) | data formatting | bytes 131072
Async XLA Ops:
  18.7 1.6 %copy-start = (f32[64,256]{1,0:T(8,128)S(1)}, f32[64,256]{1,0:T(8,128)}, u32[]{:S(2)}) copy-start(f32[64,256]{1,0:T(8,128)} %get-tuple-element.5) | copy-start | bytes 196612

commit v2 on v1

--- a/solution.py
+++ b/solution.py
@@ -9,8 +9,8 @@
 
 MESH = pl.DeviceIdType.MESH
 LANES = 128
-ROWS = 32
-WIDTHS = (3, 3, 3, 2, 2, 2, 2, 2, 2, 2, 2)
+ROWS = 24
+WIDTHS = (3, 3, 3, 2, 2, 2, 2, 2, 2, 2, 1)
 PLACES = tuple(sum(WIDTHS[:i]) for i in range(len(WIDTHS)))
 EAST, WEST, NORTH, SOUTH, NE, NW, SE, SW = range(8)
 FLAT_LIMIT = 64
@@ -58,8 +58,8 @@
     out_ice, out_ocean = refs[10:12]
     held = refs[12:22]
     (
-        ext, inv_ref, send_e, send_w, send_n, send_s, send_ne, send_nw,
-        recv_e, recv_w, recv_n, recv_s, recv_corner, wide_e, wide_w, sums,
+        ext, inv_ref, send_e, send_w, send_n, send_s,
+        recv_e, recv_w, recv_n, recv_s, recv_corner, scaled, sums,
         in_sem, send_sem, recv_sem, sum_send, sum_recv,
     ) = refs[22:]
     x = lax.axis_index("gx")
@@ -106,8 +106,8 @@
     @pl.when(bottom)
     def _():
         recv_s[...] = jnp.zeros_like(recv_s)
-        recv_corner[SE - NE] = jnp.zeros((ROWS, LANES), jnp.float32)
-        recv_corner[SW - NE] = jnp.zeros((ROWS, LANES), jnp.float32)
+        recv_corner[SE - NE] = jnp.zeros((8, LANES), jnp.float32)
+        recv_corner[SW - NE] = jnp.zeros((8, LANES), jnp.float32)
 
     for load in loads:
         load.wait()
@@ -164,8 +164,6 @@
     @pl.when(jnp.logical_not(top))
     def _():
         send_n[...] = high
-        send_ne[...] = send_e[:, cols - LANES : cols]
-        send_nw[...] = send_w[:, cols - LANES : cols]
 
     def negated(place):
         return (place < 6) | ((place >= 9) & (place < 13))
@@ -174,11 +172,6 @@
     def _():
         sign = jnp.where(negated(lane), -1.0, 1.0)
         send_n[...] = sign * flipped_lanes(flipped_rows(high))
-        row = lax.broadcasted_iota(jnp.int32, (ROWS, LANES), 0)
-        e_side = flipped_lanes(flipped_rows(send_e[:, cols - LANES : cols]))
-        send_ne[...] = jnp.where(negated(row), -e_side, e_side)
-        w_side = flipped_lanes(flipped_rows(send_w[:, cols - LANES : cols]))
-        send_nw[...] = jnp.where(negated(ROWS - 1 - row), -w_side, w_side)
 
     if flat:
         pl.semaphore_wait(barrier, total - 1)
@@ -200,20 +193,22 @@
     fold_e = lax.rem(mirror + gx - 1, gx)
     fold_w = lax.rem(mirror + 1, gx)
     corner = [recv_corner.at[k] for k in range(4)]
-    to_e = copy(send_e, recv_w, WEST, east, y)
-    to_w = copy(send_w, recv_e, EAST, west, y)
+    to_e = copy(send_e, recv_w.at[pl.ds(8, ROWS)], WEST, east, y)
+    to_w = copy(send_w, recv_e.at[pl.ds(0, ROWS)], EAST, west, y)
+    n_first, n_last = send_n.at[pl.ds(0, 8)], send_n.at[pl.ds(rows - 8, 8)]
+    s_first, s_last = send_s.at[pl.ds(0, 8)], send_s.at[pl.ds(rows - 8, 8)]
     plain_n = [
         copy(send_n, recv_s, SOUTH, x, y + 1),
-        copy(send_ne, corner[SW - NE], SW, east, y + 1),
-        copy(send_nw, corner[SE - NE], SE, west, y + 1),
+        copy(n_last, corner[SW - NE], SW, east, y + 1),
+        copy(n_first, corner[SE - NE], SE, west, y + 1),
     ]
     fold_n = copy(send_n, recv_n, NORTH, mirror, y)
-    fold_ne = copy(send_ne, corner[NE - NE], NE, fold_e, y)
-    fold_nw = copy(send_nw, corner[NW - NE], NW, fold_w, y)
+    fold_ne = copy(n_first, corner[NE - NE], NE, fold_e, y)
+    fold_nw = copy(n_last, corner[NW - NE], NW, fold_w, y)
     plain_s = [
         copy(send_s, recv_n, NORTH, x, y - 1),
-        copy(send_e.at[:, 0:LANES], corner[NW - NE], NW, east, y - 1),
-        copy(send_w.at[:, 0:LANES], corner[NE - NE], NE, west, y - 1),
+        copy(s_last, corner[NW - NE], NW, east, y - 1),
+        copy(s_first, corner[NE - NE], NE, west, y - 1),
     ]
     away_e = top & (fold_e != x)
     away_w = top & (fold_w != x)
@@ -235,11 +230,11 @@
 
     @pl.when(top & (fold_e == x))
     def _():
-        recv_corner[NE - NE] = send_ne[...]
+        recv_corner[NE - NE] = send_n[0:8]
 
     @pl.when(top & (fold_w == x))
     def _():
-        recv_corner[NW - NE] = send_nw[...]
+        recv_corner[NW - NE] = send_n[rows - 8 : rows]
 
     @pl.when(jnp.logical_not(top))
     def _():
@@ -269,21 +264,20 @@
     to_e.wait_recv()
     to_w.wait_recv()
 
-    from_n = recv_n[...]
-    from_s = recv_s[...]
-    wide_e[:, 0:cols] = recv_e[...]
-    wide_w[:, 0:cols] = recv_w[...]
-    side = lax.broadcasted_iota(jnp.int32, (ROWS, LANES), 1) < LANES // 2
-    wide_e[:, cols : cols + LANES] = jnp.where(side, recv_corner[NE - NE], recv_corner[SE - NE])
-    wide_w[:, cols : cols + LANES] = jnp.where(side, recv_corner[NW - NE], recv_corner[SW - NE])
-    upper = lax.broadcasted_iota(jnp.int32, (8, cols + LANES), 0) < 4
+    half = lax.broadcasted_iota(jnp.int32, (8, LANES), 0) < 4
+    corner_n = jnp.where(half, recv_corner[NE - NE], recv_corner[NW - NE])
+    corner_s = jnp.where(half, recv_corner[SE - NE], recv_corner[SW - NE])
+    from_n = jnp.concatenate([recv_n[...], corner_n], axis=0)
+    from_s = jnp.concatenate([recv_s[...], corner_s], axis=0)
+    near = lax.broadcasted_iota(jnp.int32, (rows + 8, LANES), 1) < LANES // 2
+    upper = lax.broadcasted_iota(jnp.int32, (8, cols), 0) < 4
     for k, place in enumerate(PLACES):
-        ext[k, 0:rows, cols : cols + LANES] = jnp.where(
-            lane < LANES // 2, rolled(from_n, -place, 1), rolled(from_s, place, 1)
-        )
-        end = ROWS - place
-        ext[k, rows : rows + 8, :] = jnp.where(
-            upper, wide_e[place : place + 8, :], wide_w[end - 8 : end, :]
+        ext[k, :, cols : cols + LANES] = jnp.where(
+            near, rolled(from_n, -place, 1), rolled(from_s, place, 1)
+        )
+        end = 8 + ROWS - place
+        ext[k, rows : rows + 8, 0:cols] = jnp.where(
+            upper, recv_e[place : place + 8, :], recv_w[end - 8 : end, :]
         )
 
     ai, ao, si, so, c = (ext[k] for k in range(6, 11))
@@ -321,7 +315,7 @@
     for k, product in enumerate(products):
         packed = jnp.where(spot == k, jnp.sum(product, keepdims=True), packed)
 
-    def exchange(slot, count, mine, device, number):
+    def exchange(slot, count, mine, device, number, work=None):
         slot[mine] = packed_now[0]
 
         def one(k):
@@ -338,11 +332,15 @@
         def _(k):
             one(k).start()
 
+        if work is not None:
+            work()
         most = slot.at[pl.ds(0, count - 1)]
         pltpu.make_async_copy(most, most, sum_recv.at[number]).wait()
-        result = jnp.sum(slot[...], axis=0)
-        pltpu.make_async_copy(most, most, sum_send.at[number]).wait()
-        return result
+        return jnp.sum(slot[...], axis=0)
+
+    def scale():
+        for k, value in enumerate((pi * ru, pi * rv, prs, pi * nu, pi * nv, pns)):
+            scaled[k] = value
 
     packed_now = [packed]
     if flat:
@@ -350,10 +348,10 @@
             other = lax.rem(me + k, total)
             return (other // gy, lax.rem(other, gy))
 
-        packed = exchange(sums, total, me, anyone, 0)
+        packed = exchange(sums, total, me, anyone, 0, scale)
     else:
         packed_now[0] = exchange(
-            sums.at[pl.ds(0, gx)], gx, x, lambda k: (lax.rem(x + k, gx), y), 0
+            sums.at[pl.ds(0, gx)], gx, x, lambda k: (lax.rem(x + k, gx), y), 0, scale
         )
         packed = exchange(
             sums.at[pl.ds(gx, gy)], gy, y, lambda k: (x, lax.rem(y + k, gy)), 1
@@ -363,10 +361,14 @@
     ]
     y1, y2 = two_by_two(s[0], s[1], s[2], s[3], s[4])
     d1, d2 = two_by_two(s[5], s[6], s[7], s[5] + s[8], s[8])
-    out_ice[0] = held[1][0] + pi * (y1 * ru + y2 * nu)
-    out_ice[1] = held[1][1] + pi * (y1 * rv + y2 * nv)
-    out_ocean[...] = held[3][...] + d1 * prs + d2 * pns
-
+    out_ice[0] = held[1][0] + y1 * scaled[0] + y2 * scaled[3]
+    out_ice[1] = held[1][1] + y1 * scaled[1] + y2 * scaled[4]
+    out_ocean[...] = held[3][...] + d1 * scaled[2] + d2 * scaled[5]
+
+    groups = [(sums, total)] if flat else [(sums.at[pl.ds(0, gx)], gx), (sums.at[pl.ds(gx, gy)], gy)]
+    for number, (slot, count) in enumerate(groups):
+        most = slot.at[pl.ds(0, count - 1)]
+        pltpu.make_async_copy(most, most, sum_send.at[number]).wait()
     to_e.wait_send()
     to_w.wait_send()
 
@@ -391,6 +393,17 @@
     def _():
         for c in plain_s:
             c.wait_send()
+
+
+def store(ice, ocean, out_ice, out_ocean, sem):
+    copies = [
+        pltpu.make_async_copy(ice, out_ice, sem.at[0]),
+        pltpu.make_async_copy(ocean, out_ocean, sem.at[1]),
+    ]
+    for c in copies:
+        c.start()
+    for c in copies:
+        c.wait()
 
 
 def solution(mesh):
@@ -402,22 +415,19 @@
         f32 = jnp.float32
         edge = pltpu.VMEM((rows, LANES), f32)
         strip = pltpu.VMEM((ROWS, cols), f32)
-        corner = pltpu.VMEM((ROWS, LANES), f32)
-        wide = pltpu.VMEM((ROWS, cols + LANES), f32)
-        return pl.pallas_call(
+        tall = pltpu.VMEM((ROWS + 8, cols), f32)
+        ice, ocean = pl.pallas_call(
             functools.partial(kernel, (gx, gy, rows, cols)),
-            out_shape=(
-                jax.ShapeDtypeStruct((2, rows, cols), f32),
-                jax.ShapeDtypeStruct((rows, cols), f32),
-            ),
+            out_shape=(pltpu.VMEM((2, rows, cols), f32), pltpu.VMEM((rows, cols), f32)),
             in_specs=[pl.BlockSpec(memory_space=pl.ANY)] * 10,
             out_specs=(pl.BlockSpec(memory_space=pltpu.VMEM),) * 2,
             scratch_shapes=[pltpu.VMEM(a.shape, a.dtype) for a in args]
             + [
                 pltpu.VMEM((len(WIDTHS), rows + 8, cols + LANES), f32),
                 pltpu.VMEM((2, rows, cols), f32),
-                strip, strip, edge, edge, corner, corner,
-                strip, strip, edge, edge, pltpu.VMEM((4, ROWS, LANES), f32), wide, wide,
+                strip, strip, edge, edge,
+                tall, tall, edge, edge, pltpu.VMEM((4, 8, LANES), f32),
+                pltpu.VMEM((6, rows, cols), f32),
                 pltpu.VMEM((slots, 1, LANES), f32),
                 pltpu.SemaphoreType.DMA((10,)),
                 pltpu.SemaphoreType.DMA((8,)),
@@ -428,6 +438,20 @@
             compiler_params=pltpu.CompilerParams(collective_id=0, has_side_effects=True),
             name="picard",
         )(*args)
+        return pl.pallas_call(
+            store,
+            out_shape=(
+                jax.ShapeDtypeStruct(ice.shape, f32),
+                jax.ShapeDtypeStruct(ocean.shape, f32),
+            ),
+            in_specs=[pl.BlockSpec(memory_space=pltpu.VMEM)] * 2,
+            out_specs=(pl.BlockSpec(memory_space=pl.ANY),) * 2,
+            scratch_shapes=[pltpu.SemaphoreType.DMA((2,))],
+            name="store",
+        )(
+            pltpu.with_memory_space_constraint(ice, pltpu.VMEM),
+            pltpu.with_memory_space_constraint(ocean, pltpu.VMEM),
+        )
 
     grid3, grid2 = P(None, "gx", "gy"), P("gx", "gy")
     return jax.shard_map(

time: 21.1 us -> 18.4 us (0.87)
  local copies, waits for them, and re-layouts: 2.23 us -> 0 us
  Pallas kernels: 18.1 us -> 17.6 us
    unnamed x4 -> x0, local copies, waits for them, and re-layouts: 2.23 us -> none
    pallas_call x1, Pallas kernels: 18.1 us -> 16.9 us  [body(): pl.pallas_call(functools.partial(kernel, (gx, gy, rows, cols)), out_shape...]
    pallas_call x0 -> x1, Pallas kernels: none -> 0.69 us  [body(): pl.pallas_call(store, out_shape=(jax.ShapeDtypeStruct(ice.shape, f32), ja...]
where the time goes in v2:
time: 18.4 us; the launch traced here: 18.2 us
  Pallas kernels  17.6 us (96%)
  between operations  0.64 us (3%)
    pallas_call x1, Pallas kernels, body(): pl.pallas_call(functools.partial(kernel, (gx, gy, rows, cols)), out_shape...  16.9 us
    pallas_call x1, Pallas kernels, body(): pl.pallas_call(store, out_shape=(jax.ShapeDtypeStruct(ice.shape, f32), ja...  0.69 us

profile of v2, /device:TPU:0, one launch (start us, length us, event | category | flops | bytes accessed | tf_op | source)
XLA Modules:
  0.0 18.2 jit_solution(15669223539015877945)
XLA Ops:
  0.6 16.9 %picard.1 = (f32[2,64,256]{2,1,0:T(8,128)S(1)}, f32[64,256]{1,0:T(8,128)S(1)}) custom-call(f32[2,64,256]{2,1,0:T(8,128)} %refs_0_.1, f32[2,64,256]{2,1,0:T(8,128)} %refs_1_.1, f32[64,256]{1,0:T(8,128)} %refs_2_.1, f32[64,256]{1,0:T(8,128)} %refs_3_.1, f32[64,256]{1,0:T(8,128)} %refs_4_.1, f32[64,256]{1,0:T(8,128)} %refs_5_.1, f32[64,256]{1,0:T(8,128)} %refs_6_.1, ...), custom_call_target="tpu_custom_call" | custom-call | tf_op jit(solution)/shard_map/picard/pallas_call | solution.py:419
  17.5 0.7 %store.1 = (f32[2,64,256]{2,1,0:T(8,128)}, f32[64,256]{1,0:T(8,128)}) custom-call(f32[2,64,256]{2,1,0:T(8,128)S(1)} %get-tuple-element.4.ice, f32[64,256]{1,0:T(8,128)S(1)} %get-tuple-element.5.ocean), custom_call_target="tpu_custom_call" | custom-call | tf_op jit(solution)/shard_map/store/pallas_call | solution.py:441

commit v3 on v2

--- a/solution.py
+++ b/solution.py
@@ -69,9 +69,6 @@
     bottom = y == 0
 
     loads = [pltpu.make_async_copy(ins[k], held[k], in_sem.at[k]) for k in range(10)]
-    for load in loads:
-        load.start()
-
     flat = total <= FLAT_LIMIT
     barrier = pltpu.get_barrier_semaphore()
 
@@ -80,10 +77,14 @@
 
     east, west = lax.rem(x + 1, gx), lax.rem(x + gx - 1, gx)
     if flat:
-        @pl.loop(1, total)
-        def _(k):
-            other = lax.rem(me + k, total)
-            greet(other // gy, lax.rem(other, gy))
+        for step in range(gx):
+            px = lax.rem(2 * gx - 1 - x + step, gx)
+            for py in range(gy):
+
+                @pl.when((px != x) | (py != y))
+                def _():
+                    greet(px, py)
+
     else:
         @pl.loop(1, gx)
         def _(k):
@@ -102,6 +103,9 @@
         def _():
             greet(east, y - 1)
             greet(west, y - 1)
+
+    for load in loads:
+        load.start()
 
     @pl.when(bottom)
     def _():
@@ -311,9 +315,14 @@
         pns * rs,
     ]
     spot = lax.broadcasted_iota(jnp.int32, (1, LANES), 1)
-    packed = jnp.zeros((1, LANES), jnp.float32)
+    spots = lax.broadcasted_iota(jnp.int32, (16, LANES), 0)
+    tall = jnp.zeros((16, LANES), jnp.float32)
     for k, product in enumerate(products):
-        packed = jnp.where(spot == k, jnp.sum(product, keepdims=True), packed)
+        halves = sum(product[:, p : p + LANES] for p in range(0, cols, LANES))
+        tall = jnp.where(spots == k, jnp.sum(halves, axis=0, keepdims=True), tall)
+    across = jnp.sum(tall, axis=1, keepdims=True)
+    diagonal = spots == lax.broadcasted_iota(jnp.int32, (16, LANES), 1)
+    packed = jnp.sum(jnp.where(diagonal, across, 0.0), axis=0, keepdims=True)
 
     def exchange(slot, count, mine, device, number, work=None):
         slot[mine] = packed_now[0]

time: 18.4 us -> 18.3 us (level)
  no operation moved by 1% of the time
where the time goes in v3:
time: 18.3 us; the launch traced here: 18.1 us
  Pallas kernels  17.5 us (96%)
  between operations  0.64 us (3%)
    pallas_call x1, Pallas kernels, body(): pl.pallas_call(functools.partial(kernel, (gx, gy, rows, cols)), out_shape...  16.8 us
    pallas_call x1, Pallas kernels, body(): pl.pallas_call(store, out_shape=(jax.ShapeDtypeStruct(ice.shape, f32), ja...  0.69 us

profile of v3, /device:TPU:0, one launch (start us, length us, event | category | flops | bytes accessed | tf_op | source)
XLA Modules:
  0.0 18.1 jit_solution(12764728005884027195)
XLA Ops:
  0.6 16.8 %picard.1 = (f32[2,64,256]{2,1,0:T(8,128)S(1)}, f32[64,256]{1,0:T(8,128)S(1)}) custom-call(f32[2,64,256]{2,1,0:T(8,128)} %refs_0_.1, f32[2,64,256]{2,1,0:T(8,128)} %refs_1_.1, f32[64,256]{1,0:T(8,128)} %refs_2_.1, f32[64,256]{1,0:T(8,128)} %refs_3_.1, f32[64,256]{1,0:T(8,128)} %refs_4_.1, f32[64,256]{1,0:T(8,128)} %refs_5_.1, f32[64,256]{1,0:T(8,128)} %refs_6_.1, ...), custom_call_target="tpu_custom_call" | custom-call | tf_op jit(solution)/shard_map/picard/pallas_call | solution.py:428
  17.4 0.7 %store.1 = (f32[2,64,256]{2,1,0:T(8,128)}, f32[64,256]{1,0:T(8,128)}) custom-call(f32[2,64,256]{2,1,0:T(8,128)S(1)} %get-tuple-element.4.ice, f32[64,256]{1,0:T(8,128)S(1)} %get-tuple-element.5.ocean), custom_call_target="tpu_custom_call" | custom-call | tf_op jit(solution)/shard_map/store/pallas_call | solution.py:450
